TPU v7x, 32 devices: a whole 2x2x4 slice. The times are simulated.
32 devices in a mesh: gx: 4 (over z), gy: 8 (over y, x, core).
Axes of the slice: x: 2, y: 2, z: 4, core: 2. Of those that a mesh axis runs over, the one named last changes fastest.
Arguments:
- policy_logp: float32 [16, 512, 4096], P('gy', 'gx'), may hold values from -2 to 0
- anchor_logp: float32 [16, 512, 4096], P('gy', 'gx'), may hold values from -2 to 0
- lengths: int32 [16, 512], P('gy', 'gx'), may hold values from 512 to 4096
- rewards: int32 [16, 512], P('gy', 'gx'), may hold values from 0 to 8
- slot_prompt: int32 [16, 512], P('gy', 'gx'), may hold values from 0 to 511, as said below
Outputs:
- token_grad: float32 [16, 512, 4096], P(None, ('gx', 'gy'))
- sample_loss: float32 [16, 512], P(None, ('gx', 'gy'))
- advantage: float32 [16, 512], P(None, ('gx', 'gy'))
Inputs may be any that keep to these rules, and one draw needn't show every extreme that they name: `slot_prompt`: for every member k and every aligned block of 128 slots, the slots of the block hold each prompt of the same block exactly once.
All inputs are finite; a program needn't handle non-finite values.
Results may differ from a plain program's by a relative error of at most 0.00002.
Values sent between devices are 32-bit elements; how exact they have to be, the bound alone decides.
A program may use at most 64 MiB of HBM per device.

v0:
```python
import jax
import jax.numpy as jnp
from jax import lax
from jax.sharding import PartitionSpec as P

kl_weight = 0.1


def score_tokens(policy, anchor, seq_len, reward, total, members, grad_scale, loss_scale):
    advantage = (members * reward - total[None, :]) / (members - 1)
    positions = lax.broadcasted_iota(jnp.float32, policy.shape, 2)
    valid = positions < seq_len[:, :, None]
    log_ratio = anchor - policy
    ratio = jnp.exp(log_ratio)
    token_term = -advantage[:, :, None] * policy + kl_weight * (ratio - log_ratio - 1.0)
    token_grad = (
        jnp.where(valid, -advantage[:, :, None] + kl_weight * (1.0 - ratio), 0.0) * grad_scale
    )
    sample_loss = jnp.sum(jnp.where(valid, token_term, 0.0), axis=2) * loss_scale
    return (token_grad, sample_loss, advantage)


def body(policy_logp, anchor_logp, lengths, rewards, slot_prompt):
    members_dev, slots, seq_slots = policy_logp.shape
    local_prompt = slot_prompt % slots
    member_rows = lax.broadcasted_iota(jnp.int32, (members_dev, slots), 0)
    slot_ids = lax.broadcasted_iota(jnp.int32, (members_dev, slots), 1)
    inverse = jnp.zeros((members_dev, slots), jnp.int32).at[member_rows, local_prompt].set(slot_ids)
    sorted_policy = jnp.take_along_axis(policy_logp, inverse[:, :, None], axis=1)
    sorted_anchor = jnp.take_along_axis(anchor_logp, inverse[:, :, None], axis=1)
    sorted_len = jnp.take_along_axis(lengths, inverse, axis=1).astype(jnp.float32)
    sorted_reward = jnp.take_along_axis(rewards, inverse, axis=1).astype(jnp.float32) * 0.25
    count_local = jnp.sum(lengths.astype(jnp.float32))
    token_total = lax.psum(count_local, ("gx", "gy"))
    members = members_dev * lax.axis_size("gy")
    samples = members * slots * lax.axis_size("gx")
    grad_scale = samples * seq_slots / token_total
    loss_scale = samples / token_total
    member_sums = jnp.sum(sorted_reward, axis=0)
    total = lax.psum(member_sums, "gy")
    token_grad, sample_loss, advantage = score_tokens(
        sorted_policy,
        sorted_anchor,
        sorted_len,
        sorted_reward,
        total,
        members,
        grad_scale,
        loss_scale,
    )
    return (
        lax.all_to_all(token_grad, "gy", split_axis=1, concat_axis=0, tiled=True),
        lax.all_to_all(sample_loss, "gy", split_axis=1, concat_axis=0, tiled=True),
        lax.all_to_all(advantage, "gy", split_axis=1, concat_axis=0, tiled=True),
    )


def solution(mesh):
    placed = (P("gy", "gx", None), P("gy", "gx", None), P("gy", "gx"), P("gy", "gx"), P("gy", "gx"))
    return jax.shard_map(
        body,
        mesh=mesh,
        in_specs=placed,
        out_specs=(P(None, ("gx", "gy"), None), P(None, ("gx", "gy")), P(None, ("gx", "gy"))),
        check_vma=False,
    )
```

profile of v0, /device:TPU:0, one launch (start us, length us, event | category | flops | bytes accessed | tf_op | source)
XLA Modules:
  0.0 189.2 jit_solution(11175729835720736867)
XLA Ops:
  0.6 0.0 copy-start
  0.7 0.7 fusion.16
  1.4 11.4 %scatter_fusion = s32[2,128]{1,0:T(2,128)S(1)} fusion(s32[2,128]{1,0:T(2,128)S(1)} %broadcast.49, s32[256]{0:T(256)S(1)} %fusion.16, s32[256]{0:T(256)S(1)} %iota_bitcast_fusion), kind=kCustom, calls=%fused_computation.4 | custom fusion | bytes 5120 | tf_op jit(solution)/shard_map/scatter | solution.py:28
  12.8 1.3 convert_reduce_fusion
  14.1 2.3 %gather_fusion = s32[256]{0:T(256)S(1)} fusion(s32[2,128]{1,0:T(2,128)} %param.11, s32[256]{0:T(256)S(1)} %get-tuple-element.10), kind=kCustom, calls=%fused_computation.clone | custom fusion | bytes 4096 | tf_op jit(solution)/shard_map/jit(take_along_axis)/gather | solution.py:31
  16.5 2.4 %gather_fusion.1 = s32[256]{0:T(256)S(1)} fusion(s32[2,128]{1,0:T(2,128)S(1)} %copy-done, s32[256]{0:T(256)S(1)} %get-tuple-element.10), kind=kCustom, calls=%fused_computation.2.clone | custom fusion | bytes 4096 | tf_op jit(solution)/shard_map/jit(take_along_axis)/gather | solution.py:32
  18.9 15.1 %psum.14 = f32[128]{0:T(128)S(1)} all-reduce(f32[128]{0:T(128)S(1)} %multiply_reduce_fusion), channel_id=1, replica_groups=mesh['gx'=4,'gy'=8] {'gy'}, use_global_device_ids=true, to_apply=%region_2.4 | all-reduce | flops 128 | bytes 1024 | tf_op jit(solution)/shard_map/psum | solution.py:40
  34.1 0.1 copy.35
  34.2 0.1 copy.34
  34.3 7.6 %gather_fusion.2 = f32[256,4096]{1,0:T(8,128)} fusion(f32[2,128,4096]{2,1,0:T(8,128)} %param.10, s32[256]{0:T(256)S(1)} %get-tuple-element.9), kind=kCustom, calls=%fused_computation.1.clone | custom fusion | bytes 8390656 | tf_op jit(solution)/shard_map/jit(take_along_axis)/gather | solution.py:30
  41.9 7.6 %gather_fusion.3 = f32[256,4096]{1,0:T(8,128)} fusion(f32[2,128,4096]{2,1,0:T(8,128)} %param.9, s32[256]{0:T(256)S(1)} %get-tuple-element.9), kind=kCustom, calls=%fused_computation.3.clone | custom fusion | bytes 8390656 | tf_op jit(solution)/shard_map/jit(take_along_axis)/gather | solution.py:29
  49.5 0.1 copy.36
  49.7 39.9 %psum.15 = f32[]{:T(128)} all-reduce(f32[]{:T(128)} %convert_reduce_fusion), channel_id=1, replica_groups=mesh['gx'=4,'gy'=8] {'gx','gy'}, use_global_device_ids=true, to_apply=%region_4.7 | all-reduce | flops 1 | bytes 8 | tf_op jit(solution)/shard_map/psum | solution.py:34
  91.0 20.6 %fusion.9 = (f32[2,128]{0,1:T(8,128)S(1)}, f32[2,128,4096]{2,0,1:T(2,128)}) fusion(f32[2,128,4096]{2,1,0:T(8,128)} %bitcast.49, pred[2,128]{0,1:T(8,128)(4,1)S(1)} %copy.36, f32[2,128]{0,1:T(8,128)S(1)} %copy.35, f32[2,128]{0,1:T(8,128)S(1)} %copy.34, f32[2,128,4096]{2,1,0:T(8,128)} %bitcast.48, f32[]{:T(128)S(6)} %div.14), kind=kLoop, calls=%fused_computation.19 | loop fusion | flops 16776960 | bytes 12586244 | tf_op jit(solution)/shard_map/reduce_sum | solution.py:19
  111.6 0.7 copy.42
  112.3 3.7 %all-to-all-start.1 = ((f32[2,8,16]{2,0,1:T(2,128)}), f32[2,8,16]{2,0,1:T(2,128)S(1)}, u32[]{:S(2)}, u32[]{:S(2)}) async-start(f32[2,8,16]{2,0,1:T(2,128)} %copy.42), calls=%async_computation.1 | async-start | bytes 16384 | tf_op jit(solution)/shard_map/all_to_all | solution.py:53
  116.0 0.1 all_to_all.46
  116.1 4.6 %all-to-all-done.1 = f32[2,8,16]{2,0,1:T(2,128)S(1)} async-done(((f32[2,8,16]{2,0,1:T(2,128)}), f32[2,8,16]{2,0,1:T(2,128)S(1)}, u32[]{:S(2)}, u32[]{:S(2)}) %all-to-all-start.1) | async-done | bytes 1056 | tf_op jit(solution)/shard_map/all_to_all | solution.py:53
  120.7 7.1 %all_to_all.53 = f32[2,8,16]{2,0,1:T(2,128)S(1)} all-to-all(f32[2,8,16]{2,0,1:T(2,128)S(1)} %copy.43), channel_id=1, replica_groups=mesh['gx'=4,'gy'=8] {'gy'}, dimensions={1} | all-to-all | bytes 2048 | tf_op jit(solution)/shard_map/all_to_all | solution.py:54
  127.8 4.5 %all-to-all-start = ((f32[2,128,4096]{2,0,1:T(2,128)}), f32[2,128,4096]{2,0,1:T(2,128)}, u32[]{:S(2)}, u32[]{:S(2)}) async-start(f32[2,128,4096]{2,0,1:T(2,128)} %get-tuple-element.8), calls=%async_computation | async-start | bytes 8388608 | tf_op jit(solution)/shard_map/all_to_all | solution.py:52
  132.4 49.1 %all-to-all-done = f32[2,128,4096]{2,0,1:T(2,128)} async-done(((f32[2,128,4096]{2,0,1:T(2,128)}), f32[2,128,4096]{2,0,1:T(2,128)}, u32[]{:S(2)}, u32[]{:S(2)}) %all-to-all-start) | async-done | bytes 4194336 | tf_op jit(solution)/shard_map/all_to_all | solution.py:52
  181.4 6.6 %copy.40 = f32[8,2,16,4096]{3,2,1,0:T(8,128)} copy(f32[8,2,16,4096]{3,1,2,0:T(2,128)} %bitcast.13) | data formatting | bytes 8388608 | tf_op jit(solution)/shard_map/all_to_all | solution.py:52
  188.0 0.6 copy.66
  188.6 0.6 copy.67
  (10 shorter events, 0.1 us)
Async XLA Ops:
  0.6 15.8 %copy-start = (s32[2,128]{1,0:T(2,128)S(1)}, s32[2,128]{1,0:T(2,128)}, u32[]{:S(2)}) copy-start(s32[2,128]{1,0:T(2,128)} %param.12) | copy-start | bytes 3076
  112.3 8.5 %all-to-all-start.1 = ((f32[2,8,16]{2,0,1:T(2,128)}), f32[2,8,16]{2,0,1:T(2,128)S(1)}, u32[]{:S(2)}, u32[]{:S(2)}) async-start(f32[2,8,16]{2,0,1:T(2,128)} %copy.42), calls=%async_computation.1 | async-start | bytes 16384 | tf_op jit(solution)/shard_map/all_to_all | solution.py:53
  127.8 53.7 %all-to-all-start = ((f32[2,128,4096]{2,0,1:T(2,128)}), f32[2,128,4096]{2,0,1:T(2,128)}, u32[]{:S(2)}, u32[]{:S(2)}) async-start(f32[2,128,4096]{2,0,1:T(2,128)} %get-tuple-element.8), calls=%async_computation | async-start | bytes 8388608 | tf_op jit(solution)/shard_map/all_to_all | solution.py:52
where the time goes:
time: 190 us; the launch traced here: 189 us
  blocking collectives  62.1 us (33%)
  waiting for transfers between devices  53.7 us (28%)
  local copies, waits for them, and re-layouts  40.4 us (21%)
  other arithmetic  22.6 us (12%)
  starting transfers between devices  8.29 us (4%)
  between operations  2.09 us (1%)
    all_to_all x1, waiting for transfers between devices, body(): lax.all_to_all(token_grad, 'gy', split_axis=1, concat_axis=0, tiled=True)  49.1 us
    psum x1, blocking collectives, body(): token_total = lax.psum(count_local, ('gx', 'gy'))  39.9 us
    reduce_sum x1, other arithmetic, score_tokens(): jnp.sum(jnp.where(valid, token_term, 0.0), axis=2) * loss_scale  20.6 us
    psum x1, blocking collectives, body(): total = lax.psum(member_sums, 'gy')  15.1 us
    scatter x1, local copies, waits for them, and re-layouts, body(): jnp.zeros((members_dev, slots), jnp.int32).at[member_rows, local_prompt]  11.4 us
    gather x1, local copies, waits for them, and re-layouts, body(): jnp.take_along_axis(policy_logp, inverse[:, :, None], axis=1)  7.64 us
    gather x1, local copies, waits for them, and re-layouts, body(): jnp.take_along_axis(anchor_logp, inverse[:, :, None], axis=1)  7.59 us
    all_to_all x1, blocking collectives, body(): lax.all_to_all(advantage, 'gy', split_axis=1, concat_axis=0, tiled=True)  7.06 us
  transfers between devices with their start and end apart: 2, of which 2 were waited for; matrix products, arithmetic and copies ran while one was open for 0% of the time, Pallas kernels for 0%

commit v1 on v0

v1 whole, which is shorter than its diff:
```python
import functools

import jax
import jax.numpy as jnp
from jax import lax
from jax.experimental import pallas as pl
from jax.experimental.pallas import tpu as pltpu
from jax.sharding import PartitionSpec as P

kl_weight = 0.1
LANES = 128
CHUNKS = 8
MESH = pl.DeviceIdType.MESH


def permuted(onehot, rows):
    high = rows.astype(jnp.bfloat16)
    rest = rows - high.astype(jnp.float32)
    middle = rest.astype(jnp.bfloat16)
    low = (rest - middle.astype(jnp.float32)).astype(jnp.bfloat16)
    dot = functools.partial(jnp.dot, preferred_element_type=jnp.float32)
    return dot(onehot, high) + dot(onehot, middle) + dot(onehot, low)


def folded(x):
    out = x[:, :LANES]
    for start in range(LANES, x.shape[1], LANES):
        out = out + x[:, start : start + LANES]
    return out


def exchange(
    n_gx, n_gy, policy_hbm, anchor_hbm, len_ref, reward_ref, prompt_ref,
    raw_hbm, heads_ref, tails_ref, ntok_ref,
    policy, anchor, sendbuf, onehot, len_col, sum_policy, sum_kl,
    heads_send, heads_recv, tails_send, tails_recv, counts,
    load_sem, send_sem, recv_sem, own_sem,
    head_send_sem, head_recv_sem, tail_send_sem, tail_recv_sem, count_send_sem, count_recv_sem,
):
    gx, gy = lax.axis_index("gx"), lax.axis_index("gy")
    members_dev, slots, seq = policy_hbm.shape
    part = slots // n_gy
    width = seq // CHUNKS

    barrier = pltpu.get_barrier_semaphore()
    for off in range(1, n_gy):
        pl.semaphore_signal(barrier, inc=1, device_id=(gx, lax.rem(gy + off, n_gy)), device_id_type=MESH)
    for off in range(1, n_gx):
        pl.semaphore_signal(barrier, inc=1, device_id=(lax.rem(gx + off, n_gx), gy), device_id_type=MESH)

    def loads(c):
        cols = pl.ds(pl.multiple_of(c * width, LANES), width)
        return (
            pltpu.make_async_copy(policy_hbm.at[:, :, cols], policy.at[c], load_sem.at[0, c]),
            pltpu.make_async_copy(anchor_hbm.at[:, :, cols], anchor.at[c], load_sem.at[1, c]),
        )

    for c in range(CHUNKS):
        for copy in loads(c):
            copy.start()

    sublane = lax.broadcasted_iota(jnp.int32, (slots, slots), 0)
    lane = lax.broadcasted_iota(jnp.int32, (slots, slots), 1)
    column = lax.broadcasted_iota(jnp.int32, (slots, LANES), 1)
    local_tokens = jnp.sum(len_ref[...].astype(jnp.float32))
    for m in range(members_dev):
        seq_len = len_ref[m : m + 1, :].astype(jnp.float32)
        reward = reward_ref[m : m + 1, :].astype(jnp.float32) * 0.25
        match = sublane == lax.rem(prompt_ref[m : m + 1, :], slots)
        onehot[m] = jnp.where(match, 1.0, 0.0).astype(jnp.bfloat16)
        len_col[m] = jnp.broadcast_to(
            jnp.sum(jnp.where(sublane == lane, seq_len, 0.0), axis=1, keepdims=True), (slots, LANES)
        )
        sorted_len = jnp.sum(jnp.where(match, seq_len, 0.0), axis=1, keepdims=True)
        sorted_reward = jnp.sum(jnp.where(match, reward, 0.0), axis=1, keepdims=True)
        heads_send[m] = jnp.where(
            column == 0, sorted_len, jnp.where(column == 1, sorted_reward, local_tokens)
        )
    sum_policy[...] = jnp.zeros_like(sum_policy)
    sum_kl[...] = jnp.zeros_like(sum_kl)

    def compute(c):
        for copy in loads(c):
            copy.wait()
        positions = (lax.broadcasted_iota(jnp.int32, (slots, width), 1) + c * width).astype(jnp.float32)
        for m in range(members_dev):
            pol = policy[c, m]
            log_ratio = anchor[c, m] - pol
            ratio = jnp.exp(log_ratio)
            valid = positions < len_col[m][:, :1]
            sum_policy[m] += folded(jnp.where(valid, pol, 0.0))
            sum_kl[m] += folded(jnp.where(valid, kl_weight * (ratio - log_ratio - 1.0), 0.0))
            sendbuf[c, m] = permuted(onehot[m], kl_weight * (1.0 - ratio))

    def rows_of(device):
        return pl.ds(pl.multiple_of(device * part, part), part)

    my_members = pl.ds(gy * members_dev, members_dev)

    def sends(c):
        cols = pl.ds(pl.multiple_of(c * width, LANES), width)
        copies = []
        for off in range(1, n_gy):
            peer = lax.rem(gy + off, n_gy)
            copies.append(
                pltpu.make_async_remote_copy(
                    src_ref=sendbuf.at[c, :, rows_of(peer), :],
                    dst_ref=raw_hbm.at[my_members, :, cols],
                    send_sem=send_sem.at[off - 1],
                    recv_sem=recv_sem.at[off - 1],
                    device_id=(gx, peer),
                    device_id_type=MESH,
                )
            )
        return copies

    def own(c):
        cols = pl.ds(pl.multiple_of(c * width, LANES), width)
        return pltpu.make_async_copy(
            sendbuf.at[c, :, rows_of(gy), :], raw_hbm.at[my_members, :, cols], own_sem.at[c]
        )

    def small_sends(src, dst, send, recv):
        copies = []
        for off in range(1, n_gy):
            peer = lax.rem(gy + off, n_gy)
            copies.append(
                pltpu.make_async_remote_copy(
                    src_ref=src.at[:, rows_of(peer), :],
                    dst_ref=dst.at[my_members],
                    send_sem=send.at[off - 1],
                    recv_sem=recv.at[off - 1],
                    device_id=(gx, peer),
                    device_id_type=MESH,
                )
            )
        copies.append(pltpu.make_async_copy(src.at[:, rows_of(gy), :], dst.at[my_members], send.at[n_gy - 1]))
        return copies

    def count_sends():
        return [
            pltpu.make_async_remote_copy(
                src_ref=counts.at[0],
                dst_ref=counts.at[off],
                send_sem=count_send_sem.at[off - 1],
                recv_sem=count_recv_sem.at[off - 1],
                device_id=(lax.rem(gx + off, n_gx), gy),
                device_id_type=MESH,
            )
            for off in range(1, n_gx)
        ]

    compute(0)
    pl.semaphore_wait(barrier, n_gy - 1 + n_gx - 1)
    head_copies = small_sends(heads_send, heads_recv, head_send_sem, head_recv_sem)
    for copy in head_copies:
        copy.start()

    def step(c, carry):
        for copy in sends(c - 1):
            copy.start()
        own(c - 1).start()
        compute(c)
        return carry

    lax.fori_loop(1, CHUNKS, step, 0)
    for copy in sends(CHUNKS - 1):
        copy.start()
    own(CHUNKS - 1).start()

    for m in range(members_dev):
        s1 = jnp.sum(permuted(onehot[m], sum_policy[m]), axis=1, keepdims=True)
        s2 = jnp.sum(permuted(onehot[m], sum_kl[m]), axis=1, keepdims=True)
        tails_send[m] = jnp.where(column == 0, s1, s2)
    for copy in head_copies:
        copy.wait()
    tokens = jnp.zeros((8, LANES), jnp.float32)
    for source in range(n_gy):
        tokens = tokens + heads_recv[source * members_dev, :8, :]
    counts[0] = tokens
    heads_ref[...] = heads_recv[...]
    tail_copies = small_sends(tails_send, tails_recv, tail_send_sem, tail_recv_sem)
    for copy in tail_copies:
        copy.start()
    count_copies = count_sends()
    for copy in count_copies:
        copy.start()
    for copy in count_copies:
        copy.wait()
    ntok_ref[...] = jnp.sum(counts[...], axis=0)
    for copy in tail_copies:
        copy.wait()
    tails_ref[...] = tails_recv[...]
    for c in range(CHUNKS):
        own(c).wait()
    for off in range(1, n_gy):
        source = lax.rem(gy + n_gy - off, n_gy)
        landed = raw_hbm.at[pl.ds(source * members_dev, members_dev)]
        pltpu.make_async_copy(landed, landed, recv_sem.at[off - 1]).wait()
        pltpu.make_async_copy(landed, landed, send_sem.at[off - 1]).wait()


def finish(samples, raw, heads, tails, ntok, grad, loss, adv):
    members, part = heads.shape[0], heads.shape[1]
    group, _, seq = raw.shape
    step = pl.program_id(0)
    tokens = ntok[:1, 2:3]
    total = jnp.sum(heads[...], axis=0)

    def advantage_of(head):
        return (members * head[:, :, 1:2] - total[None, :, 1:2]) / (members - 1)

    head = heads[pl.ds(step * group, group)]
    positions = lax.broadcasted_iota(jnp.int32, (group, part, seq), 2).astype(jnp.float32)
    scale = (samples * seq / tokens)[None]
    grad[...] = jnp.where(positions < head[:, :, :1], raw[...] - advantage_of(head), 0.0) * scale

    @pl.when(step == 0)
    def _():
        shape = (members, part, LANES)
        eye = lax.broadcasted_iota(jnp.int32, shape, 1) == lax.broadcasted_iota(jnp.int32, shape, 2)
        advantage = advantage_of(heads[...])
        value = (tails[:, :, 1:2] - advantage * tails[:, :, :1]) * (samples / tokens)[None]
        loss[...] = jnp.sum(jnp.where(eye, value, 0.0), axis=1)[:, :part]
        adv[...] = jnp.sum(jnp.where(eye, advantage, 0.0), axis=1)[:, :part]


def body(n_gx, n_gy, policy_logp, anchor_logp, lengths, rewards, slot_prompt):
    members_dev, slots, seq = policy_logp.shape
    members, part = members_dev * n_gy, slots // n_gy
    f32 = jnp.float32
    chunked = (CHUNKS, members_dev, slots, seq // CHUNKS)
    small = (members, part, LANES)
    any_spec = pl.BlockSpec(memory_space=pl.ANY)
    vmem_spec = pl.BlockSpec(memory_space=pltpu.VMEM)
    dma = pltpu.SemaphoreType.DMA
    raw, heads, tails, ntok = pl.pallas_call(
        functools.partial(exchange, n_gx, n_gy),
        out_shape=(
            jax.ShapeDtypeStruct((members, part, seq), f32),
            jax.ShapeDtypeStruct(small, f32),
            jax.ShapeDtypeStruct(small, f32),
            jax.ShapeDtypeStruct((8, LANES), f32),
        ),
        in_specs=[any_spec, any_spec, vmem_spec, vmem_spec, vmem_spec],
        out_specs=(any_spec, vmem_spec, vmem_spec, vmem_spec),
        scratch_shapes=[
            pltpu.VMEM(chunked, f32),
            pltpu.VMEM(chunked, f32),
            pltpu.VMEM(chunked, f32),
            pltpu.VMEM((members_dev, slots, slots), jnp.bfloat16),
            pltpu.VMEM((members_dev, slots, LANES), f32),
            pltpu.VMEM((members_dev, slots, LANES), f32),
            pltpu.VMEM((members_dev, slots, LANES), f32),
            pltpu.VMEM((members_dev, slots, LANES), f32),
            pltpu.VMEM(small, f32),
            pltpu.VMEM((members_dev, slots, LANES), f32),
            pltpu.VMEM(small, f32),
            pltpu.VMEM((n_gx, 8, LANES), f32),
            dma((2, CHUNKS)),
            dma((n_gy - 1,)),
            dma((n_gy - 1,)),
            dma((CHUNKS,)),
            dma((n_gy,)),
            dma((n_gy - 1,)),
            dma((n_gy,)),
            dma((n_gy - 1,)),
            dma((n_gx - 1,)),
            dma((n_gx - 1,)),
        ],
        compiler_params=pltpu.CompilerParams(collective_id=0, has_side_effects=True),
    )(policy_logp, anchor_logp, lengths, rewards, slot_prompt)
    group = 2
    samples = members * slots * n_gx
    block = pl.BlockSpec((group, part, seq), lambda i: (i, 0, 0))
    whole = lambda shape: pl.BlockSpec(shape, lambda i: (0,) * len(shape))
    return pl.pallas_call(
        functools.partial(finish, samples),
        grid=(members // group,),
        out_shape=(
            jax.ShapeDtypeStruct((members, part, seq), f32),
            jax.ShapeDtypeStruct((members, part), f32),
            jax.ShapeDtypeStruct((members, part), f32),
        ),
        in_specs=[block, whole(small), whole(small), whole((8, LANES))],
        out_specs=(block, whole((members, part)), whole((members, part))),
    )(raw, heads, tails, ntok)


def solution(mesh):
    placed = (P("gy", "gx", None), P("gy", "gx", None), P("gy", "gx"), P("gy", "gx"), P("gy", "gx"))
    return jax.shard_map(
        functools.partial(body, mesh.shape["gx"], mesh.shape["gy"]),
        mesh=mesh,
        in_specs=placed,
        out_specs=(P(None, ("gx", "gy"), None), P(None, ("gx", "gy")), P(None, ("gx", "gy"))),
        check_vma=False,
    )
```

time: 190 us -> 65.8 us (0.35)
  Pallas kernels: 0 us -> 64.8 us
  blocking collectives: 62.1 us -> 0 us
  waiting for transfers between devices: 53.7 us -> 0 us
  local copies, waits for them, and re-layouts: 40.4 us -> 0 us
  other arithmetic: 22.6 us -> 0 us
  starting transfers between devices: 8.29 us -> 0 us
    pallas_call x0 -> x2, Pallas kernels: none -> 64.8 us  [the longest x1 57.3 us: body(): pl.pallas_call(functools.partial(exchange, n_gx, n_gy), out_shape=(jax.Sh...]
    psum x2 -> x0, blocking collectives: 55.1 us -> none  [the longest x1 39.9 us: body(): token_total = lax.psum(count_local, ('gx', 'gy'))]
    all_to_all x2 -> x0, waiting for transfers between devices: 53.7 us -> none  [the longest x1 49.1 us: body(): lax.all_to_all(token_grad, 'gy', split_axis=1, concat_axis=0, tiled=True)]
    reduce_sum x3 -> x0, other arithmetic: 21.9 us -> none  [the longest x1 20.6 us: score_tokens(): jnp.sum(jnp.where(valid, token_term, 0.0), axis=2) * loss_scale]
    gather x4 -> x0, local copies, waits for them, and re-layouts: 20 us -> none  [the longest x1 7.64 us: body(): jnp.take_along_axis(policy_logp, inverse[:, :, None], axis=1)]
    scatter x1 -> x0, local copies, waits for them, and re-layouts: 11.4 us -> none  [body(): jnp.zeros((members_dev, slots), jnp.int32).at[member_rows, local_prompt]]
    all_to_all x2 -> x0, starting transfers between devices: 8.29 us -> none  [the longest x1 4.55 us: body(): lax.all_to_all(token_grad, 'gy', split_axis=1, concat_axis=0, tiled=True)]
    all_to_all x1 -> x0, blocking collectives: 7.06 us -> none  [body(): lax.all_to_all(advantage, 'gy', split_axis=1, concat_axis=0, tiled=True)]
  transfers between devices with their start and end apart: 2 -> 0, of which waited for: 2 -> 0; matrix products, arithmetic and copies ran while one was open for 0% -> 0% of each run, Pallas kernels for 0% -> 0%
where the time goes in v1:
time: 65.8 us; the launch traced here: 65.5 us
  Pallas kernels  64.8 us (98%)
    pallas_call x1, Pallas kernels, body(): pl.pallas_call(functools.partial(exchange, n_gx, n_gy), out_shape=(jax.Sh...  57.3 us
    pallas_call x1, Pallas kernels, body(): pl.pallas_call(functools.partial(finish, samples), grid=(members // group...  7.54 us

profile of v1, /device:TPU:0, one launch (start us, length us, event | category | flops | bytes accessed | tf_op | source)
XLA Modules:
  0.0 65.5 jit_solution(13964693354417021566)
XLA Ops:
  0.6 57.3 %shard_map.76 = (f32[16,16,4096]{2,1,0:T(8,128)}, f32[16,16,128]{2,1,0:T(8,128)}, f32[16,16,128]{2,1,0:T(8,128)}, f32[8,128]{1,0:T(8,128)}) custom-call(f32[2,128,4096]{2,1,0:T(8,128)} %policy_hbm.1, f32[2,128,4096]{2,1,0:T(8,128)} %anchor_hbm.1, s32[2,128]{1,0:T(2,128)} %len_ref.1, s32[2,128]{1,0:T(2,128)} %reward_ref.1, s32[2,128]{1,0:T(2,128)} %prompt_ref.1), custom_call_target="tpu_custom_call" | custom-call | tf_op jit(solution)/shard_map/pallas_call | solution.py:237
  57.9 7.5 %shard_map.77 = (f32[16,16,4096]{2,1,0:T(8,128)}, f32[16,16]{1,0:T(8,128)}, f32[16,16]{1,0:T(8,128)}) custom-call(f32[16,16,4096]{2,1,0:T(8,128)} %get-tuple-element.7.raw, f32[16,16,128]{2,1,0:T(8,128)} %get-tuple-element.8.heads, f32[16,16,128]{2,1,0:T(8,128)} %get-tuple-element.9.tails, f32[8,128]{1,0:T(8,128)} %get-tuple-element.10.ntok), custom_call_target="tpu_custom_call" | custom-call | tf_op jit(solution)/shard_map/pallas_call | solution.py:277

commit v2 on v1

--- a/solution.py
+++ b/solution.py
@@ -11,6 +11,21 @@
 LANES = 128
 CHUNKS = 8
 MESH = pl.DeviceIdType.MESH
+
+
+def partner(index, off, count):
+    out, bit = index, 1
+    while bit < count:
+        if off & bit:
+            out = out + bit - 2 * bit * lax.rem(index // bit, 2)
+        bit *= 2
+    return out
+
+
+def offsets_by_distance(count):
+    far = max(bin(off // 2).count("1") for off in range(1, count))
+    near = [off for off in range(1, count) if bin(off // 2).count("1") < far]
+    return near, [off for off in range(1, count) if off not in near]
 
 
 def permuted(onehot, rows):
@@ -42,9 +57,10 @@
     part = slots // n_gy
     width = seq // CHUNKS
 
+    near, far = offsets_by_distance(n_gy)
     barrier = pltpu.get_barrier_semaphore()
     for off in range(1, n_gy):
-        pl.semaphore_signal(barrier, inc=1, device_id=(gx, lax.rem(gy + off, n_gy)), device_id_type=MESH)
+        pl.semaphore_signal(barrier, inc=1, device_id=(gx, partner(gy, off, n_gy)), device_id_type=MESH)
     for off in range(1, n_gx):
         pl.semaphore_signal(barrier, inc=1, device_id=(lax.rem(gx + off, n_gx), gy), device_id_type=MESH)
 
@@ -97,11 +113,11 @@
 
     my_members = pl.ds(gy * members_dev, members_dev)
 
-    def sends(c):
+    def sends(c, offs):
         cols = pl.ds(pl.multiple_of(c * width, LANES), width)
         copies = []
-        for off in range(1, n_gy):
-            peer = lax.rem(gy + off, n_gy)
+        for off in offs:
+            peer = partner(gy, off, n_gy)
             copies.append(
                 pltpu.make_async_remote_copy(
                     src_ref=sendbuf.at[c, :, rows_of(peer), :],
@@ -123,7 +139,7 @@
     def small_sends(src, dst, send, recv):
         copies = []
         for off in range(1, n_gy):
-            peer = lax.rem(gy + off, n_gy)
+            peer = partner(gy, off, n_gy)
             copies.append(
                 pltpu.make_async_remote_copy(
                     src_ref=src.at[:, rows_of(peer), :],
@@ -157,15 +173,22 @@
         copy.start()
 
     def step(c, carry):
-        for copy in sends(c - 1):
+        for copy in sends(c - 1, near):
             copy.start()
         own(c - 1).start()
         compute(c)
         return carry
 
     lax.fori_loop(1, CHUNKS, step, 0)
-    for copy in sends(CHUNKS - 1):
+    for copy in sends(CHUNKS - 1, near):
         copy.start()
+
+    def far_step(c, carry):
+        for copy in sends(c, far):
+            copy.start()
+        return carry
+
+    lax.fori_loop(0, CHUNKS, far_step, 0)
     own(CHUNKS - 1).start()
 
     for m in range(members_dev):
@@ -194,7 +217,7 @@
     for c in range(CHUNKS):
         own(c).wait()
     for off in range(1, n_gy):
-        source = lax.rem(gy + n_gy - off, n_gy)
+        source = partner(gy, off, n_gy)
         landed = raw_hbm.at[pl.ds(source * members_dev, members_dev)]
         pltpu.make_async_copy(landed, landed, recv_sem.at[off - 1]).wait()
         pltpu.make_async_copy(landed, landed, send_sem.at[off - 1]).wait()
@@ -202,7 +225,7 @@
 
 def finish(samples, raw, heads, tails, ntok, grad, loss, adv):
     members, part = heads.shape[0], heads.shape[1]
-    group, _, seq = raw.shape
+    group, _, seq = grad.shape
     step = pl.program_id(0)
     tokens = ntok[:1, 2:3]
     total = jnp.sum(heads[...], axis=0)
@@ -213,7 +236,7 @@
     head = heads[pl.ds(step * group, group)]
     positions = lax.broadcasted_iota(jnp.int32, (group, part, seq), 2).astype(jnp.float32)
     scale = (samples * seq / tokens)[None]
-    grad[...] = jnp.where(positions < head[:, :, :1], raw[...] - advantage_of(head), 0.0) * scale
+    grad[...] = jnp.where(positions < head[:, :, :1], raw[pl.ds(step * group, group)] - advantage_of(head), 0.0) * scale
 
     @pl.when(step == 0)
     def _():
@@ -231,19 +254,20 @@
     f32 = jnp.float32
     chunked = (CHUNKS, members_dev, slots, seq // CHUNKS)
     small = (members, part, LANES)
+    hbm_spec = pl.BlockSpec(memory_space=pltpu.HBM)
     any_spec = pl.BlockSpec(memory_space=pl.ANY)
     vmem_spec = pl.BlockSpec(memory_space=pltpu.VMEM)
     dma = pltpu.SemaphoreType.DMA
     raw, heads, tails, ntok = pl.pallas_call(
         functools.partial(exchange, n_gx, n_gy),
         out_shape=(
-            jax.ShapeDtypeStruct((members, part, seq), f32),
-            jax.ShapeDtypeStruct(small, f32),
-            jax.ShapeDtypeStruct(small, f32),
-            jax.ShapeDtypeStruct((8, LANES), f32),
+            pltpu.VMEM((members, part, seq), f32),
+            pltpu.VMEM(small, f32),
+            pltpu.VMEM(small, f32),
+            pltpu.VMEM((8, LANES), f32),
         ),
-        in_specs=[any_spec, any_spec, vmem_spec, vmem_spec, vmem_spec],
-        out_specs=(any_spec, vmem_spec, vmem_spec, vmem_spec),
+        in_specs=[hbm_spec, hbm_spec, vmem_spec, vmem_spec, vmem_spec],
+        out_specs=(vmem_spec, vmem_spec, vmem_spec, vmem_spec),
         scratch_shapes=[
             pltpu.VMEM(chunked, f32),
             pltpu.VMEM(chunked, f32),
@@ -268,9 +292,9 @@
             dma((n_gx - 1,)),
             dma((n_gx - 1,)),
         ],
-        compiler_params=pltpu.CompilerParams(collective_id=0, has_side_effects=True),
+        compiler_params=pltpu.CompilerParams(collective_id=0, has_side_effects=True, vmem_limit_bytes=56 * 2**20),
     )(policy_logp, anchor_logp, lengths, rewards, slot_prompt)
-    group = 2
+    group = 4
     samples = members * slots * n_gx
     block = pl.BlockSpec((group, part, seq), lambda i: (i, 0, 0))
     whole = lambda shape: pl.BlockSpec(shape, lambda i: (0,) * len(shape))
@@ -282,8 +306,9 @@
             jax.ShapeDtypeStruct((members, part), f32),
             jax.ShapeDtypeStruct((members, part), f32),
         ),
-        in_specs=[block, whole(small), whole(small), whole((8, LANES))],
+        in_specs=[vmem_spec] * 4,
         out_specs=(block, whole((members, part)), whole((members, part))),
+        compiler_params=pltpu.CompilerParams(vmem_limit_bytes=32 * 2**20),
     )(raw, heads, tails, ntok)
 
 

time: 65.8 us -> 60.8 us (0.924)
  Pallas kernels: 64.8 us -> 60 us
    pallas_call x1, Pallas kernels: 7.54 us -> 3.1 us  [body(): pl.pallas_call(functools.partial(finish, samples), grid=(members // group...]
where the time goes in v2:
time: 60.8 us; the launch traced here: 60.7 us
  Pallas kernels  60 us (99%)
  between operations  0.64 us (1%)
    pallas_call x1, Pallas kernels, body(): pl.pallas_call(functools.partial(exchange, n_gx, n_gy), out_shape=(pltpu....  56.9 us
    pallas_call x1, Pallas kernels, body(): pl.pallas_call(functools.partial(finish, samples), grid=(members // group...  3.1 us

profile of v2, /device:TPU:0, one launch (start us, length us, event | category | flops | bytes accessed | tf_op | source)
XLA Modules:
  0.0 60.7 jit_solution(8011471315278648031)
XLA Ops:
  0.6 56.9 %shard_map.76 = (f32[16,16,4096]{2,1,0:T(8,128)S(1)}, f32[16,16,128]{2,1,0:T(8,128)S(1)}, f32[16,16,128]{2,1,0:T(8,128)S(1)}, f32[8,128]{1,0:T(8,128)S(1)}) custom-call(f32[2,128,4096]{2,1,0:T(8,128)} %policy_hbm.1, f32[2,128,4096]{2,1,0:T(8,128)} %anchor_hbm.1, s32[2,128]{1,0:T(2,128)} %len_ref.1, s32[2,128]{1,0:T(2,128)} %reward_ref.1, s32[2,128]{1,0:T(2,128)} %prompt_ref.1), custom_call_target="tpu_custom_call" | custom-call | tf_op jit(solution)/shard_map/pallas_call | solution.py:261
  57.6 3.1 %shard_map.77 = (f32[16,16,4096]{2,1,0:T(8,128)}, f32[16,16]{1,0:T(8,128)}, f32[16,16]{1,0:T(8,128)}) custom-call(f32[16,16,4096]{2,1,0:T(8,128)S(1)} %get-tuple-element.7.raw, f32[16,16,128]{2,1,0:T(8,128)S(1)} %get-tuple-element.8.heads, f32[16,16,128]{2,1,0:T(8,128)S(1)} %get-tuple-element.9.tails, f32[8,128]{1,0:T(8,128)S(1)} %get-tuple-element.10.ntok), custom_call_target="tpu_custom_call" | custom-call | tf_op jit(solution)/shard_map/pallas_call | solution.py:301

commit v3 on v2

--- a/solution.py
+++ b/solution.py
@@ -223,29 +223,29 @@
         pltpu.make_async_copy(landed, landed, send_sem.at[off - 1]).wait()
 
 
-def finish(samples, raw, heads, tails, ntok, grad, loss, adv):
-    members, part = heads.shape[0], heads.shape[1]
-    group, _, seq = grad.shape
-    step = pl.program_id(0)
+def finish(samples, raw, heads, tails, ntok, grad, loss, adv, done, done_sem):
+    members, part, seq = raw.shape
     tokens = ntok[:1, 2:3]
     total = jnp.sum(heads[...], axis=0)
-
-    def advantage_of(head):
-        return (members * head[:, :, 1:2] - total[None, :, 1:2]) / (members - 1)
-
-    head = heads[pl.ds(step * group, group)]
-    positions = lax.broadcasted_iota(jnp.int32, (group, part, seq), 2).astype(jnp.float32)
-    scale = (samples * seq / tokens)[None]
-    grad[...] = jnp.where(positions < head[:, :, :1], raw[pl.ds(step * group, group)] - advantage_of(head), 0.0) * scale
-
-    @pl.when(step == 0)
-    def _():
-        shape = (members, part, LANES)
-        eye = lax.broadcasted_iota(jnp.int32, shape, 1) == lax.broadcasted_iota(jnp.int32, shape, 2)
-        advantage = advantage_of(heads[...])
-        value = (tails[:, :, 1:2] - advantage * tails[:, :, :1]) * (samples / tokens)[None]
-        loss[...] = jnp.sum(jnp.where(eye, value, 0.0), axis=1)[:, :part]
-        adv[...] = jnp.sum(jnp.where(eye, advantage, 0.0), axis=1)[:, :part]
+    advantage = (members * heads[:, :, 1:2] - total[None, :, 1:2]) / (members - 1)
+    positions = lax.broadcasted_iota(jnp.int32, (part, seq), 1).astype(jnp.float32)
+    scale = samples * seq / tokens
+
+    def store(k):
+        return pltpu.make_async_copy(done.at[k], grad.at[k], done_sem.at[k])
+
+    for k in range(members):
+        done[k] = jnp.where(positions < heads[k, :, :1], raw[k] - advantage[k], 0.0) * scale
+        if k > 0:
+            store(k - 1).start()
+    shape = (members, part, LANES)
+    eye = lax.broadcasted_iota(jnp.int32, shape, 1) == lax.broadcasted_iota(jnp.int32, shape, 2)
+    store(members - 1).start()
+    value = (tails[:, :, 1:2] - advantage * tails[:, :, :1]) * (samples / tokens)[None]
+    loss[...] = jnp.sum(jnp.where(eye, value, 0.0), axis=1)[:, :part]
+    adv[...] = jnp.sum(jnp.where(eye, advantage, 0.0), axis=1)[:, :part]
+    for k in range(members):
+        store(k).wait()
 
 
 def body(n_gx, n_gy, policy_logp, anchor_logp, lengths, rewards, slot_prompt):
@@ -255,7 +255,6 @@
     chunked = (CHUNKS, members_dev, slots, seq // CHUNKS)
     small = (members, part, LANES)
     hbm_spec = pl.BlockSpec(memory_space=pltpu.HBM)
-    any_spec = pl.BlockSpec(memory_space=pl.ANY)
     vmem_spec = pl.BlockSpec(memory_space=pltpu.VMEM)
     dma = pltpu.SemaphoreType.DMA
     raw, heads, tails, ntok = pl.pallas_call(
@@ -294,20 +293,17 @@
         ],
         compiler_params=pltpu.CompilerParams(collective_id=0, has_side_effects=True, vmem_limit_bytes=56 * 2**20),
     )(policy_logp, anchor_logp, lengths, rewards, slot_prompt)
-    group = 4
     samples = members * slots * n_gx
-    block = pl.BlockSpec((group, part, seq), lambda i: (i, 0, 0))
-    whole = lambda shape: pl.BlockSpec(shape, lambda i: (0,) * len(shape))
     return pl.pallas_call(
         functools.partial(finish, samples),
-        grid=(members // group,),
         out_shape=(
             jax.ShapeDtypeStruct((members, part, seq), f32),
             jax.ShapeDtypeStruct((members, part), f32),
             jax.ShapeDtypeStruct((members, part), f32),
         ),
         in_specs=[vmem_spec] * 4,
-        out_specs=(block, whole((members, part)), whole((members, part))),
+        out_specs=(hbm_spec, vmem_spec, vmem_spec),
+        scratch_shapes=[pltpu.VMEM((members, part, seq), f32), dma((members,))],
         compiler_params=pltpu.CompilerParams(vmem_limit_bytes=32 * 2**20),
     )(raw, heads, tails, ntok)
 

time: 60.8 us -> 60.7 us (level)
  no operation moved by 1% of the time
where the time goes in v3:
time: 60.7 us; the launch traced here: 60.6 us
  Pallas kernels  59.9 us (99%)
  between operations  0.64 us (1%)
    pallas_call x1, Pallas kernels, body(): pl.pallas_call(functools.partial(exchange, n_gx, n_gy), out_shape=(pltpu....  56.9 us
    pallas_call x1, Pallas kernels, body(): pl.pallas_call(functools.partial(finish, samples), out_shape=(jax.ShapeDt...  2.99 us

profile of v3, /device:TPU:0, one launch (start us, length us, event | category | flops | bytes accessed | tf_op | source)
XLA Modules:
  0.0 60.6 jit_solution(14453147557305371173)
XLA Ops:
  0.6 56.9 %shard_map.76 = (f32[16,16,4096]{2,1,0:T(8,128)S(1)}, f32[16,16,128]{2,1,0:T(8,128)S(1)}, f32[16,16,128]{2,1,0:T(8,128)S(1)}, f32[8,128]{1,0:T(8,128)S(1)}) custom-call(f32[2,128,4096]{2,1,0:T(8,128)} %policy_hbm.1, f32[2,128,4096]{2,1,0:T(8,128)} %anchor_hbm.1, s32[2,128]{1,0:T(2,128)} %len_ref.1, s32[2,128]{1,0:T(2,128)} %reward_ref.1, s32[2,128]{1,0:T(2,128)} %prompt_ref.1), custom_call_target="tpu_custom_call" | custom-call | tf_op jit(solution)/shard_map/pallas_call | solution.py:260
  57.6 3.0 %shard_map.77 = (f32[16,16,4096]{2,1,0:T(8,128)}, f32[16,16]{1,0:T(8,128)}, f32[16,16]{1,0:T(8,128)}) custom-call(f32[16,16,4096]{2,1,0:T(8,128)S(1)} %get-tuple-element.7.raw, f32[16,16,128]{2,1,0:T(8,128)S(1)} %get-tuple-element.8.heads, f32[16,16,128]{2,1,0:T(8,128)S(1)} %get-tuple-element.9.tails, f32[8,128]{1,0:T(8,128)S(1)} %get-tuple-element.10.ntok), custom_call_target="tpu_custom_call" | custom-call | tf_op jit(solution)/shard_map/pallas_call | solution.py:297
